TPU v7x, 512 devices: a whole 4x8x8 slice. The times are simulated.
512 devices in a mesh: ka: 16 (over y_hi, x), band: 32 (over y_lo, z, core).
Axes of the slice: x: 4, y: 8 (y_hi: 4, y_lo: 2; y = y_hi * 2 + y_lo), z: 8, core: 2. Of those that a mesh axis runs over, the one named last changes fastest.
Arguments:
- targets: bfloat16 [16, 32, 24, 24, 128], P('ka', 'band'), may hold values from -6 to 6
- occupied: bfloat16 [16, 64, 24, 24, 128], P('ka', 'band'), may hold values from -6 to 6
- wavevectors: int32 [16, 3], replicated, may hold values from 0 to 3
- umklapp: int32 [16, 2, 3], P('ka'), may hold values from -1 to 1
- owners: int32 [16, 2, 2], P('ka'), may hold values from 0 to 31
Outputs:
- exchange: bfloat16 [16, 32, 24, 24, 128], P('ka', 'band')
All inputs are finite; a program needn't handle non-finite values.
Results may differ from a plain program's by a relative error of at most 0.017.
Values may be sent and summed in bfloat16 or wider, within the bound.
No kernel may reach another device: no remote copies, remote signals or barrier semaphores. Data moves between devices by JAX's collectives and lax.ppermute only.
A program may use at most 64 MiB of HBM per device.

v0:
```python
import functools
import math

import jax
import jax.numpy as jnp
import ml_dtypes
import numpy as np
from jax import lax
from jax.experimental import pallas as pl
from jax.experimental.pallas import tpu as pltpu
from jax.sharding import PartitionSpec as P


OCC_DEV = 2
STEPS = 2
KGRID = 4

screening_sq = 0.16
spacing = 0.25
prefactor = -0.5

LANES = 128


def shift_ka_by_core(block, sign):
    n_ka, n_band = lax.axis_size("ka"), lax.axis_size("band")
    route = []
    for k in range(n_ka):
        for b in range(n_band):
            to = (k + sign * (1 + b % 2)) % n_ka
            route.append((k * n_band + b, to * n_band + b))
    return lax.ppermute(block, ("ka", "band"), route)


def band_groups():
    along_yz = [[yz * 2 + c for yz in range(16)] for c in range(2)]
    cores = [[yz * 2 + c for c in range(2)] for yz in range(16)]
    return along_yz, cores


def rounded_tables(length):
    indices = np.arange(length)
    angles = (indices[:, None] * indices[None, :] % length) * (2.0 * math.pi / length)
    rounded = lambda t: t.astype(np.float32).astype(ml_dtypes.bfloat16).astype(np.float64)
    return rounded(np.cos(angles)), rounded(np.sin(angles))


def half_plane(grid_y, grid_z):
    rows = np.arange(grid_y * grid_z)
    opposite = (-(rows // grid_z)) % grid_y * grid_z + (-(rows % grid_z)) % grid_z
    chosen = rows[rows <= opposite]
    return chosen, opposite[chosen], (opposite[chosen] != chosen).astype(np.float32)


def half_padded(grid_y, grid_z):
    return -(-len(half_plane(grid_y, grid_z)[0]) // 64) * 64


def plane_tables(grid_y, grid_z):
    cos_y, sin_y = rounded_tables(grid_y)
    cos_z, sin_z = rounded_tables(grid_z)
    chosen = half_plane(grid_y, grid_z)[0]
    rows, half = grid_y * grid_z, half_padded(grid_y, grid_z)
    width = 2 * half
    there = np.zeros((2, half, width), np.float32)
    there[0, : len(chosen), :rows] = (np.kron(cos_y, cos_z) - np.kron(sin_y, sin_z))[chosen]
    there[1, : len(chosen), :rows] = (np.kron(sin_y, cos_z) + np.kron(cos_y, sin_z))[chosen]
    back = there[:, :, :rows].transpose(2, 0, 1).reshape(rows, 2 * half)
    return np.concatenate([there.reshape(2 * half, width), back]).astype(ml_dtypes.bfloat16)


def plane_frequencies(grid_y, grid_z):
    chosen, opposite, differ = half_plane(grid_y, grid_z)
    table = np.zeros((half_padded(grid_y, grid_z), 8), np.float32)
    for column, (which, length) in enumerate(
        [
            (chosen // grid_z, grid_y),
            (chosen % grid_z, grid_z),
            (opposite // grid_z, grid_y),
            (opposite % grid_z, grid_z),
        ]
    ):
        table[: len(chosen), column] = np.where(which * 2 < length, which, which - length)
    table[: len(chosen), 4] = differ
    return table


def line_table(grid_x, sign):
    cosine, sine = rounded_tables(grid_x)
    re_in = np.concatenate([cosine, -sign * sine], axis=1)
    im_in = np.concatenate([sign * sine, cosine], axis=1)
    straight = np.concatenate([re_in, im_in], axis=0)
    turned = np.concatenate([sign * straight[:, grid_x:], -sign * straight[:, :grid_x]], axis=1)
    return np.concatenate([straight, turned], axis=1).astype(np.float32).astype(ml_dtypes.bfloat16)


def coulomb_kernel(grid, wavevectors, umklapp, frequencies, out):
    grid_x, grid_y, grid_z = grid
    width = out.shape[-1]
    cells = float(grid_x * grid_y * grid_z)
    k = lax.axis_index("ka")
    k_total = lax.axis_size("ka")

    def square(signed, length, shift):
        wavenumber = 2.0 * math.pi / (length * spacing) * (signed + shift)
        return wavenumber * wavenumber

    lane = lax.broadcasted_iota(jnp.int32, (1, width), 1)
    index_x = jnp.where(lane < grid_x, lane, lane - grid_x)
    signed_x = jnp.where(index_x * 2 < grid_x, index_x, index_x - grid_x).astype(jnp.float32)
    for s in range(out.shape[0]):
        visit = lax.rem(k + (k_total - s - 1), k_total)
        shift = [
            (wavevectors[a, k] - wavevectors[a, visit]).astype(jnp.float32) / KGRID
            + umklapp[0, s, a].astype(jnp.float32)
            for a in range(3)
        ]
        line = square(signed_x, grid_x, shift[0])
        kern = []
        for column in (0, 2):
            plane = square(frequencies[:, column : column + 1], grid_y, shift[1]) + square(
                frequencies[:, column + 1 : column + 2], grid_z, shift[2]
            )
            kern.append((4.0 * math.pi / cells) / (plane + line + screening_sq))
        opposite = kern[1] * frequencies[:, 4:5]
        out[s, 0] = kern[0] + opposite
        out[s, 1] = kern[0] - opposite


def coulomb(wavevectors, umklapp, grid_x, grid_y, grid_z):
    smem = pl.BlockSpec(memory_space=pltpu.SMEM)
    vmem = pl.BlockSpec(memory_space=pltpu.VMEM)
    half = half_padded(grid_y, grid_z)
    return pl.pallas_call(
        functools.partial(coulomb_kernel, (grid_x, grid_y, grid_z)),
        out_shape=jax.ShapeDtypeStruct((STEPS, 2, half, 2 * grid_x), jnp.float32),
        in_specs=[smem, smem, vmem],
        out_specs=vmem,
    )(wavevectors.T, umklapp, jnp.asarray(plane_frequencies(grid_y, grid_z)))


def exchange_kernel(
    visitors, psi, planes, lines, kern, out, dense, given, even, odd, pair, stack, plane
):
    rows, turn = out.shape[0], LANES // 2
    width = planes.shape[1]
    half = width // 2
    terms = STEPS * OCC_DEV
    left = lax.broadcasted_iota(jnp.int32, (1, LANES), 1) < turn
    chunk = 96

    def lanes(term):
        return pl.ds(term * LANES, LANES)

    given[:, pl.ds(rows, width - rows), :] = jnp.zeros(
        (2, width - rows, terms * LANES), given.dtype
    )
    for first in range(0, rows, chunk):
        own = psi[pl.ds(first, chunk), :].astype(jnp.float32)
        turned = pltpu.roll(own, turn, 1)
        with_phi = jnp.where(left, own, -turned)
        with_turned = jnp.where(left, turned, own)
        for term in range(terms):
            phi = visitors[term, pl.ds(first, chunk), :].astype(jnp.float32)
            density = phi * with_phi + pltpu.roll(phi, turn, 1) * with_turned
            dense[pl.ds(term * rows + first, chunk), :] = density.astype(jnp.bfloat16)
    for term in range(terms):
        both = jnp.dot(
            dense[pl.ds(term * rows, rows), :],
            lines[:, : 2 * LANES],
            preferred_element_type=jnp.float32,
        ).astype(jnp.bfloat16)
        given[0, pl.ds(0, rows), lanes(term)] = both[:, :LANES]
        given[1, pl.ds(0, rows), lanes(term)] = both[:, LANES:]

    even[...] = jnp.dot(planes[:half], given[0], preferred_element_type=jnp.float32)
    odd[...] = jnp.dot(planes[half:width], given[1], preferred_element_type=jnp.float32)
    for term in range(terms):
        total, differ = kern[term // OCC_DEV, 0], kern[term // OCC_DEV, 1]
        e, o = even[:, lanes(term)], odd[:, lanes(term)]
        pair[0, pl.ds(term * half, half), :] = (e * total + o * differ).astype(jnp.bfloat16)
        pair[1, pl.ds(term * half, half), :] = (e * differ + o * total).astype(jnp.bfloat16)
    for part in range(2):
        turned = jnp.dot(
            pair[part],
            lines[:, (2 + part) * LANES : (3 + part) * LANES],
            preferred_element_type=jnp.float32,
        ).astype(jnp.bfloat16)
        for term in range(terms):
            stack[pl.ds(part * half, half), lanes(term)] = turned[term * half : (term + 1) * half]

    plane[...] = jnp.dot(planes[width:], stack[...], preferred_element_type=jnp.float32)
    for first in range(0, rows, chunk):
        straight = crossed = None
        for term in range(terms):
            phi = visitors[term, pl.ds(first, chunk), :].astype(jnp.float32)
            potential = plane[pl.ds(first, chunk), lanes(term)]
            one, two = phi * potential, pltpu.roll(phi, turn, 1) * potential
            straight = one if term == 0 else straight + one
            crossed = two if term == 0 else crossed + two
        total = jnp.where(
            left, straight - pltpu.roll(straight, turn, 1), crossed + pltpu.roll(crossed, turn, 1)
        )
        out[pl.ds(first, chunk), :] = (prefactor * total).astype(out.dtype)


def apply_exchange(visitors, psi, kern, grid_x, grid_y, grid_z):
    rows = grid_y * grid_z
    terms = STEPS * OCC_DEV
    planes = plane_tables(grid_y, grid_z)
    lines = np.concatenate([line_table(grid_x, 1.0), line_table(grid_x, -1.0)], axis=1)
    width = planes.shape[1]
    half = width // 2
    vmem = pl.BlockSpec(memory_space=pltpu.VMEM)
    return pl.pallas_call(
        exchange_kernel,
        out_shape=jax.ShapeDtypeStruct((rows, LANES), jnp.bfloat16),
        in_specs=[vmem] * 5,
        out_specs=vmem,
        scratch_shapes=[
            pltpu.VMEM((terms * rows, LANES), jnp.bfloat16),
            pltpu.VMEM((2, width, terms * LANES), jnp.bfloat16),
            pltpu.VMEM((half, terms * LANES), jnp.float32),
            pltpu.VMEM((half, terms * LANES), jnp.float32),
            pltpu.VMEM((2, terms * half, LANES), jnp.bfloat16),
            pltpu.VMEM((2 * half, terms * LANES), jnp.bfloat16),
            pltpu.VMEM((rows, terms * LANES), jnp.float32),
        ],
        compiler_params=pltpu.CompilerParams(vmem_limit_bytes=16 * 1024 * 1024),
    )(
        visitors,
        psi,
        jnp.asarray(planes),
        jnp.asarray(lines),
        kern,
    )


def exchange(targets, occupied, wavevectors, umklapp, owners):
    resident = targets[0, 0]
    grid_y, grid_z, last_width = resident.shape
    grid_x = last_width // 2
    rows = grid_y * grid_z
    band = lax.axis_index("band")
    core, slot = band % 2, band // 16
    along_yz, cores = band_groups()
    n_yz = len(cores)

    flat = occupied[0].reshape(n_yz, OCC_DEV * rows // n_yz, last_width)
    spread = lax.all_to_all(flat, "band", 0, 0, tiled=True, axis_index_groups=along_yz)
    spread = lax.all_gather(spread, "band", axis_index_groups=cores)

    wanted = shift_ka_by_core(owners[0], -1)
    owner = lax.dynamic_slice(wanted, (core, slot), (1, 1), allow_negative_indices=False)[0, 0]
    spread = spread.reshape((2 * n_yz,) + flat.shape[1:])
    place = jnp.bitwise_and(owner, 1) * n_yz + lax.shift_right_logical(owner, 1)
    chosen = lax.dynamic_slice(
        spread, (place, 0, 0), (1,) + flat.shape[1:], allow_negative_indices=False
    )[0]
    mine = shift_ka_by_core(chosen, 1)

    kern = coulomb(wavevectors, umklapp, grid_x, grid_y, grid_z)
    column = jnp.broadcast_to(mine[None], (n_yz,) + mine.shape)
    column = lax.all_to_all(column, "band", 0, 0, tiled=True, axis_index_groups=along_yz)
    visitors = lax.all_gather(column, "band", axis_index_groups=cores)
    visitors = visitors.reshape(STEPS * OCC_DEV, rows, last_width)

    result = apply_exchange(
        visitors,
        resident.reshape(rows, last_width),
        kern,
        grid_x,
        grid_y,
        grid_z,
    )
    return result.reshape((1, 1) + resident.shape)


def solution(mesh):
    placed = (
        P("ka", "band", None, None, None),
        P("ka", "band", None, None, None),
        P(),
        P("ka", None, None),
        P("ka", None, None),
    )
    return jax.shard_map(
        exchange,
        mesh=mesh,
        in_specs=placed,
        out_specs=P("ka", "band", None, None, None),
        check_vma=False,
    )
```

profile of v0, /device:TPU:1, one launch (start us, length us, event | category | flops | bytes accessed | tf_op | source)
XLA Modules:
  0.0 60.6 jit_solution(17594523390917049177)
XLA Ops:
  0.0 12.0 %all-to-all-start = ((bf16[16,72,128]{2,1,0:T(8,128)(2,1)}), bf16[16,72,128]{2,1,0:T(8,128)(2,1)S(1)}, u32[]{:S(2)}, u32[]{:S(2)}) async-start(bf16[16,72,128]{2,1,0:T(8,128)(2,1)} %bitcast.11), calls=%async_computation | async-start | bytes 589824 | tf_op jit(solution)/shard_map/all_to_all | solution.py:250
  12.0 7.4 %collective-permute-start = (s32[2,2]{1,0:T(2,128)}, s32[2,2]{1,0:T(2,128)S(1)}, u32[]{:S(2)}, u32[]{:S(2)}) collective-permute-start(s32[2,2]{1,0:T(2,128)} %bitcast.13), channel_id=1, source_target_pairs={{0,480},{1,449},{2,482},{3,451},{4,484},{5,453},{6,486},{7,455},{8... | collective-permute-start | bytes 56 | tf_op jit(solution)/shard_map/ppermute | solution.py:32
  19.5 0.9 %collective-permute-done = s32[2,2]{1,0:T(2,128)S(1)} collective-permute-done((s32[2,2]{1,0:T(2,128)}, s32[2,2]{1,0:T(2,128)S(1)}, u32[]{:S(2)}, u32[]{:S(2)}) %collective-permute-start) | collective-permute-done | bytes 48 | tf_op jit(solution)/shard_map/ppermute | solution.py:32
  20.3 0.6 dynamic_slice.6
  22.2 0.0 copy-start.1
  22.2 0.0 copy-start.2
  22.3 0.0 copy-start.3
  22.3 0.0 all-to-all-done
  22.3 3.8 %all-gather = bf16[32,72,128]{2,1,0:T(8,128)(2,1)S(1)} all-gather(bf16[16,72,128]{2,1,0:T(8,128)(2,1)S(1)} %all-to-all-done), channel_id=2, replica_groups={{0,1},{2,3},{4,5},{6,7},{8,9},{10,11},{12,13},{14,15},{16,17},{18,19},{..., dimensions={0}, use_global_device_ids=true | all-gather | bytes 884736 | tf_op jit(solution)/shard_map/all_gather | solution.py:251
  26.1 4.5 %collective-permute-start.1 = (bf16[72,128]{1,0:T(8,128)(2,1)S(1)}, bf16[72,128]{1,0:T(8,128)(2,1)S(1)}, u32[]{:S(2)}, u32[]{:S(2)}) collective-permute-start(bf16[72,128]{1,0:T(8,128)(2,1)S(1)} %dynamic-slice_bitcast_fusion), channel_id=1, source_target_pairs={{0,32},{1,65},{2,34},{3,67},{4,36},{5,69},{6,38},{7,71},{8,40},{9,... | collective-permute-start | bytes 55304 | tf_op jit(solution)/shard_map/ppermute | solution.py:32
  30.6 4.5 %collective-permute-done.1 = bf16[72,128]{1,0:T(8,128)(2,1)S(1)} collective-permute-done((bf16[72,128]{1,0:T(8,128)(2,1)S(1)}, bf16[72,128]{1,0:T(8,128)(2,1)S(1)}, u32[]{:S(2)}, u32[]{:S(2)}) %collective-permute-start.1) | collective-permute-done | bytes 18464 | tf_op jit(solution)/shard_map/ppermute | solution.py:32
  35.1 0.7 %broadcast_in_dim.2 = bf16[16,72,128]{2,1,0:T(8,128)(2,1)} broadcast(bf16[72,128]{1,0:T(8,128)(2,1)S(1)} %collective-permute-done.1), dimensions={1,2} | broadcast | bytes 313344 | tf_op jit(solution)/shard_map/broadcast_in_dim | solution.py:263
  35.8 7.8 %all-to-all-start.1 = ((bf16[16,72,128]{2,1,0:T(8,128)(2,1)}), bf16[16,72,128]{2,1,0:T(8,128)(2,1)S(1)}, u32[]{:S(2)}, u32[]{:S(2)}) async-start(bf16[16,72,128]{2,1,0:T(8,128)(2,1)} %broadcast_in_dim.2), calls=%async_computation.1 | async-start | bytes 589824 | tf_op jit(solution)/shard_map/all_to_all | solution.py:264
  43.6 2.3 %shard_map.82.kern = f32[2,2,320,128]{3,2,1,0:T(8,128)} custom-call(s32[3,16]{1,0:T(4,128)} %bitcast.12, s32[1,2,3]{2,1,0:T(2,128)} %umklapp.1, f32[320,8]{1,0:T(8,128)} %constant.44.clone.frequencies), custom_call_target="tpu_custom_call" | custom-call | tf_op jit(solution)/shard_map/pallas_call | solution.py:134
  45.9 6.0 %all-to-all-done.1 = bf16[16,72,128]{2,1,0:T(8,128)(2,1)S(1)} async-done(((bf16[16,72,128]{2,1,0:T(8,128)(2,1)}), bf16[16,72,128]{2,1,0:T(8,128)(2,1)S(1)}, u32[]{:S(2)}, u32[]{:S(2)}) %all-to-all-start.1) | async-done | bytes 294944 | tf_op jit(solution)/shard_map/all_to_all | solution.py:264
  51.9 4.7 %all-gather.1 = bf16[32,72,128]{2,1,0:T(8,128)(2,1)S(1)} all-gather(bf16[16,72,128]{2,1,0:T(8,128)(2,1)S(1)} %all-to-all-done.1), channel_id=3, replica_groups={{0,1},{2,3},{4,5},{6,7},{8,9},{10,11},{12,13},{14,15},{16,17},{18,19},{..., dimensions={0}, use_global_device_ids=true | all-gather | bytes 884736 | tf_op jit(solution)/shard_map/all_gather | solution.py:265
  56.6 0.0 copy-done.1
  56.6 0.0 copy-done.2
  56.6 0.0 copy-done.3
  56.6 0.0 copy-start
  56.6 1.1 %copy-done = f32[2,2,320,128]{3,2,1,0:T(8,128)S(1)} copy-done((f32[2,2,320,128]{3,2,1,0:T(8,128)S(1)}, f32[2,2,320,128]{3,2,1,0:T(8,128)}, u32[]{:S(2)}) %copy-start) | copy-done | bytes 655384
  57.7 2.8 %shard_map.83 = bf16[576,128]{1,0:T(8,128)(2,1)} custom-call(bf16[4,576,128]{2,1,0:T(8,128)(2,1)S(1)} %bitcast.9, bf16[576,128]{1,0:T(8,128)(2,1)S(1)} %bitcast.10, bf16[1216,640]{1,0:T(8,128)(2,1)S(1)} %copy-done.1, bf16[128,512]{1,0:T(8,128)(2,1)S(1)} %copy-done.3, f32[2,2,320,128]{3,2,1,0:T(8,128)S(1)} %copy-done), custom_call_target="tpu_custom_call" | custom-call | tf_op jit(solution)/shard_map/pallas_call | solution.py:215
  (1 shorter events, 0.0 us)
Async XLA Ops:
  0.0 22.3 %all-to-all-start = ((bf16[16,72,128]{2,1,0:T(8,128)(2,1)}), bf16[16,72,128]{2,1,0:T(8,128)(2,1)S(1)}, u32[]{:S(2)}, u32[]{:S(2)}) async-start(bf16[16,72,128]{2,1,0:T(8,128)(2,1)} %bitcast.11), calls=%async_computation | async-start | bytes 589824 | tf_op jit(solution)/shard_map/all_to_all | solution.py:250
  12.0 8.4 %collective-permute-start = (s32[2,2]{1,0:T(2,128)}, s32[2,2]{1,0:T(2,128)S(1)}, u32[]{:S(2)}, u32[]{:S(2)}) collective-permute-start(s32[2,2]{1,0:T(2,128)} %bitcast.13), channel_id=1, source_target_pairs={{0,480},{1,449},{2,482},{3,451},{4,484},{5,453},{6,486},{7,455},{8... | collective-permute-start | bytes 56 | tf_op jit(solution)/shard_map/ppermute | solution.py:32
  22.2 34.4 %copy-start.1 = (bf16[1216,640]{1,0:T(8,128)(2,1)S(1)}, bf16[1216,640]{1,0:T(8,128)(2,1)}, u32[]{:S(2)}) copy-start(bf16[1216,640]{1,0:T(8,128)(2,1)} %constant.45.clone.planes) | copy-start | bytes 4669444
  22.2 34.4 %copy-start.2 = (bf16[1,1,24,24,128]{4,3,2,1,0:T(8,128)(2,1)S(1)}, bf16[1,1,24,24,128]{4,3,2,1,0:T(8,128)(2,1)}, u32[]{:S(2)}) copy-start(bf16[1,1,24,24,128]{4,3,2,1,0:T(8,128)(2,1)} %param.8) | copy-start | bytes 442372
  22.3 34.4 %copy-start.3 = (bf16[128,512]{1,0:T(8,128)(2,1)S(1)}, bf16[128,512]{1,0:T(8,128)(2,1)}, u32[]{:S(2)}) copy-start(bf16[128,512]{1,0:T(8,128)(2,1)} %constant.46.clone.lines) | copy-start | bytes 393220
  26.1 9.0 %collective-permute-start.1 = (bf16[72,128]{1,0:T(8,128)(2,1)S(1)}, bf16[72,128]{1,0:T(8,128)(2,1)S(1)}, u32[]{:S(2)}, u32[]{:S(2)}) collective-permute-start(bf16[72,128]{1,0:T(8,128)(2,1)S(1)} %dynamic-slice_bitcast_fusion), channel_id=1, source_target_pairs={{0,32},{1,65},{2,34},{3,67},{4,36},{5,69},{6,38},{7,71},{8,40},{9,... | collective-permute-start | bytes 55304 | tf_op jit(solution)/shard_map/ppermute | solution.py:32
  35.8 16.1 %all-to-all-start.1 = ((bf16[16,72,128]{2,1,0:T(8,128)(2,1)}), bf16[16,72,128]{2,1,0:T(8,128)(2,1)S(1)}, u32[]{:S(2)}, u32[]{:S(2)}) async-start(bf16[16,72,128]{2,1,0:T(8,128)(2,1)} %broadcast_in_dim.2), calls=%async_computation.1 | async-start | bytes 589824 | tf_op jit(solution)/shard_map/all_to_all | solution.py:264
  56.6 1.1 %copy-start = (f32[2,2,320,128]{3,2,1,0:T(8,128)S(1)}, f32[2,2,320,128]{3,2,1,0:T(8,128)}, u32[]{:S(2)}) copy-start(f32[2,2,320,128]{3,2,1,0:T(8,128)} %shard_map.82.kern) | copy-start | bytes 1966084
where the time goes:
time: 61 us; the launch traced here: 60.6 us
  starting transfers between devices  31.7 us (52%)
  waiting for transfers between devices  11.3 us (19%)
  blocking collectives  8.52 us (14%)
  Pallas kernels  5.18 us (8%)
  local copies, waits for them, and re-layouts  2.43 us (4%)
  between operations  1.39 us (2%)
    all_to_all x1, starting transfers between devices, exchange(): lax.all_to_all(flat, 'band', 0, 0, tiled=True, axis_index_groups=along_yz)  12 us
    ppermute x2, starting transfers between devices, shift_ka_by_core(): return lax.ppermute(block, ('ka', 'band'), route)  12 us
    all_to_all x1, starting transfers between devices, exchange(): lax.all_to_all(column, 'band', 0, 0, tiled=True, axis_index_groups=along_yz)  7.77 us
    all_to_all x1, waiting for transfers between devices, exchange(): lax.all_to_all(column, 'band', 0, 0, tiled=True, axis_index_groups=along_yz)  5.96 us
    ppermute x2, waiting for transfers between devices, shift_ka_by_core(): return lax.ppermute(block, ('ka', 'band'), route)  5.38 us
    all_gather x1, blocking collectives, exchange(): visitors = lax.all_gather(column, 'band', axis_index_groups=cores)  4.74 us
    all_gather x1, blocking collectives, exchange(): spread = lax.all_gather(spread, 'band', axis_index_groups=cores)  3.78 us
    pallas_call x1, Pallas kernels, apply_exchange(): pl.pallas_call(exchange_kernel, out_shape=jax.ShapeDtypeStruct((rows, LAN...  2.84 us
  transfers between devices with their start and end apart: 4, of which 3 were waited for; matrix products, arithmetic and copies ran while one was open for 1% of the time, Pallas kernels for 4%

commit v1 on v0

--- a/solution.py
+++ b/solution.py
@@ -250,12 +250,12 @@
     spread = lax.all_to_all(flat, "band", 0, 0, tiled=True, axis_index_groups=along_yz)
     spread = lax.all_gather(spread, "band", axis_index_groups=cores)
 
-    wanted = shift_ka_by_core(owners[0], -1)
-    owner = lax.dynamic_slice(wanted, (core, slot), (1, 1), allow_negative_indices=False)[0, 0]
+    places = jnp.bitwise_and(owners[0], 1) * n_yz + lax.shift_right_logical(owners[0], 1)
+    place = lax.dynamic_slice(places, (core, slot), (1, 1), allow_negative_indices=False)
+    wanted = shift_ka_by_core(place, -1)
     spread = spread.reshape((2 * n_yz,) + flat.shape[1:])
-    place = jnp.bitwise_and(owner, 1) * n_yz + lax.shift_right_logical(owner, 1)
     chosen = lax.dynamic_slice(
-        spread, (place, 0, 0), (1,) + flat.shape[1:], allow_negative_indices=False
+        spread, (wanted[0, 0], 0, 0), (1,) + flat.shape[1:], allow_negative_indices=False
     )[0]
     mine = shift_ka_by_core(chosen, 1)
 

time: 61 us -> 60.3 us (0.989)
  blocking collectives: 8.52 us -> 10.7 us
  starting transfers between devices: 31.7 us -> 30 us
  between operations: 1.39 us -> 0.08 us
  waiting for transfers between devices: 11.3 us -> 10.3 us
  other arithmetic: 0 us -> 0.69 us
  local copies, waits for them, and re-layouts: 2.43 us -> 3.06 us
    all_to_all x1, starting transfers between devices: 7.77 us -> 5.77 us  [exchange(): lax.all_to_all(column, 'band', 0, 0, tiled=True, axis_index_groups=along_yz)]
    all_gather x1, blocking collectives: 3.78 us -> 5.06 us  [exchange(): spread = lax.all_gather(spread, 'band', axis_index_groups=cores)]
    ppermute x2, waiting for transfers between devices: 5.38 us -> 4.36 us  [shift_ka_by_core(): return lax.ppermute(block, ('ka', 'band'), route)]
    all_gather x1, blocking collectives: 4.74 us -> 5.61 us  [exchange(): visitors = lax.all_gather(column, 'band', axis_index_groups=cores)]
    add x0 -> x1, other arithmetic: none -> 0.69 us  [exchange(): jnp.bitwise_and(owners[0], 1) * n_yz + lax.shift_right_logical(owners[0], 1)]
    squeeze x1, local copies, waits for them, and re-layouts: 0.01 us -> 0.63 us  [exchange(): lax.dynamic_slice(spread, (wanted[0, 0], 0, 0), (1,) + flat.shape[1:], al...]
  transfers between devices with their start and end apart: 4 -> 4, of which waited for: 3 -> 2; matrix products, arithmetic and copies ran while one was open for 1% -> 2% of each run, Pallas kernels for 4% -> 4%
where the time goes in v1:
time: 60.3 us; the launch traced here: 59.9 us
  starting transfers between devices  30 us (50%)
  blocking collectives  10.7 us (18%)
  waiting for transfers between devices  10.3 us (17%)
  Pallas kernels  5.18 us (9%)
  local copies, waits for them, and re-layouts  3.06 us (5%)
  other arithmetic  0.69 us (1%)
    ppermute x2, starting transfers between devices, shift_ka_by_core(): return lax.ppermute(block, ('ka', 'band'), route)  12.2 us
    all_to_all x1, starting transfers between devices, exchange(): lax.all_to_all(flat, 'band', 0, 0, tiled=True, axis_index_groups=along_yz)  12 us
    all_to_all x1, waiting for transfers between devices, exchange(): lax.all_to_all(column, 'band', 0, 0, tiled=True, axis_index_groups=along_yz)  5.89 us
    all_to_all x1, starting transfers between devices, exchange(): lax.all_to_all(column, 'band', 0, 0, tiled=True, axis_index_groups=along_yz)  5.77 us
    all_gather x1, blocking collectives, exchange(): visitors = lax.all_gather(column, 'band', axis_index_groups=cores)  5.61 us
    all_gather x1, blocking collectives, exchange(): spread = lax.all_gather(spread, 'band', axis_index_groups=cores)  5.06 us
    ppermute x2, waiting for transfers between devices, shift_ka_by_core(): return lax.ppermute(block, ('ka', 'band'), route)  4.36 us
    pallas_call x1, Pallas kernels, apply_exchange(): pl.pallas_call(exchange_kernel, out_shape=jax.ShapeDtypeStruct((rows, LAN...  2.84 us
  transfers between devices with their start and end apart: 4, of which 2 were waited for; matrix products, arithmetic and copies ran while one was open for 2% of the time, Pallas kernels for 4%

profile of v1, /device:TPU:1, one launch (start us, length us, event | category | flops | bytes accessed | tf_op | source)
XLA Modules:
  0.0 59.9 jit_solution(6546783381480781722)
XLA Ops:
  0.0 12.0 %all-to-all-start = ((bf16[16,72,128]{2,1,0:T(8,128)(2,1)}), bf16[16,72,128]{2,1,0:T(8,128)(2,1)S(1)}, u32[]{:S(2)}, u32[]{:S(2)}) async-start(bf16[16,72,128]{2,1,0:T(8,128)(2,1)} %bitcast.11), calls=%async_computation | async-start | bytes 589824 | tf_op jit(solution)/shard_map/all_to_all | solution.py:250
  12.0 0.7 %shift-right-logical_add_fusion = s32[1,2,2]{2,1,0:T(2,128)S(1)} fusion(s32[1,2,2]{2,1,0:T(2,128)} %param.12), kind=kLoop, calls=%fused_computation.1 | loop fusion | flops 16 | bytes 32 | tf_op jit(solution)/shard_map/add | solution.py:253
  12.7 0.6 constant_dynamic-slice_fusion
  13.3 0.0 copy-start.1
  13.3 0.0 copy-start.2
  13.3 0.0 copy-start.3
  13.3 7.6 %collective-permute-start = (s32[1,1]{1,0:T(1,128)}, s32[1,1]{1,0:T(1,128)}, u32[]{:S(2)}, u32[]{:S(2)}) collective-permute-start(s32[1,1]{1,0:T(1,128)} %bitcast.1), channel_id=1, source_target_pairs={{0,480},{1,449},{2,482},{3,451},{4,484},{5,453},{6,486},{7,455},{8... | collective-permute-start | bytes 20 | tf_op jit(solution)/shard_map/ppermute | solution.py:32
  20.9 0.0 all-to-all-done
  20.9 5.1 %all-gather = bf16[32,72,128]{2,1,0:T(8,128)(2,1)S(1)} all-gather(bf16[16,72,128]{2,1,0:T(8,128)(2,1)S(1)} %all-to-all-done), channel_id=2, replica_groups={{0,1},{2,3},{4,5},{6,7},{8,9},{10,11},{12,13},{14,15},{16,17},{18,19},{..., dimensions={0}, use_global_device_ids=true | all-gather | bytes 884736 | tf_op jit(solution)/shard_map/all_gather | solution.py:251
  25.9 0.0 collective-permute-done
  25.9 0.6 %dynamic-slice_bitcast_fusion = bf16[72,128]{1,0:T(8,128)(2,1)S(1)} fusion(bf16[32,72,128]{2,1,0:T(8,128)(2,1)S(1)} %all-gather, s32[]{:T(128)} %bitcast.2), kind=kLoop, calls=%fused_computation | loop fusion | bytes 36868 | tf_op jit(solution)/shard_map/squeeze | solution.py:257
  26.6 4.7 %collective-permute-start.1 = (bf16[72,128]{1,0:T(8,128)(2,1)S(1)}, bf16[72,128]{1,0:T(8,128)(2,1)S(1)}, u32[]{:S(2)}, u32[]{:S(2)}) collective-permute-start(bf16[72,128]{1,0:T(8,128)(2,1)S(1)} %dynamic-slice_bitcast_fusion), channel_id=1, source_target_pairs={{0,32},{1,65},{2,34},{3,67},{4,36},{5,69},{6,38},{7,71},{8,40},{9,... | collective-permute-start | bytes 55304 | tf_op jit(solution)/shard_map/ppermute | solution.py:32
  31.2 4.4 %collective-permute-done.1 = bf16[72,128]{1,0:T(8,128)(2,1)S(1)} collective-permute-done((bf16[72,128]{1,0:T(8,128)(2,1)S(1)}, bf16[72,128]{1,0:T(8,128)(2,1)S(1)}, u32[]{:S(2)}, u32[]{:S(2)}) %collective-permute-start.1) | collective-permute-done | bytes 18464 | tf_op jit(solution)/shard_map/ppermute | solution.py:32
  35.6 0.7 %broadcast_in_dim.2 = bf16[16,72,128]{2,1,0:T(8,128)(2,1)} broadcast(bf16[72,128]{1,0:T(8,128)(2,1)S(1)} %collective-permute-done.1), dimensions={1,2} | broadcast | bytes 313344 | tf_op jit(solution)/shard_map/broadcast_in_dim | solution.py:263
  36.3 5.8 %all-to-all-start.1 = ((bf16[16,72,128]{2,1,0:T(8,128)(2,1)}), bf16[16,72,128]{2,1,0:T(8,128)(2,1)S(1)}, u32[]{:S(2)}, u32[]{:S(2)}) async-start(bf16[16,72,128]{2,1,0:T(8,128)(2,1)} %broadcast_in_dim.2), calls=%async_computation.1 | async-start | bytes 589824 | tf_op jit(solution)/shard_map/all_to_all | solution.py:264
  42.1 2.3 %shard_map.82.kern = f32[2,2,320,128]{3,2,1,0:T(8,128)} custom-call(s32[3,16]{1,0:T(4,128)} %bitcast.12, s32[1,2,3]{2,1,0:T(2,128)} %umklapp.1, f32[320,8]{1,0:T(8,128)} %constant.42.clone.frequencies), custom_call_target="tpu_custom_call" | custom-call | tf_op jit(solution)/shard_map/pallas_call | solution.py:134
  44.4 5.9 %all-to-all-done.1 = bf16[16,72,128]{2,1,0:T(8,128)(2,1)S(1)} async-done(((bf16[16,72,128]{2,1,0:T(8,128)(2,1)}), bf16[16,72,128]{2,1,0:T(8,128)(2,1)S(1)}, u32[]{:S(2)}, u32[]{:S(2)}) %all-to-all-start.1) | async-done | bytes 294944 | tf_op jit(solution)/shard_map/all_to_all | solution.py:264
  50.3 5.6 %all-gather.1 = bf16[32,72,128]{2,1,0:T(8,128)(2,1)S(1)} all-gather(bf16[16,72,128]{2,1,0:T(8,128)(2,1)S(1)} %all-to-all-done.1), channel_id=3, replica_groups={{0,1},{2,3},{4,5},{6,7},{8,9},{10,11},{12,13},{14,15},{16,17},{18,19},{..., dimensions={0}, use_global_device_ids=true | all-gather | bytes 884736 | tf_op jit(solution)/shard_map/all_gather | solution.py:265
  55.9 0.0 copy-done.1
  56.0 0.0 copy-done.2
  56.0 0.0 copy-done.3
  56.0 0.0 copy-start
  56.0 1.1 %copy-done = f32[2,2,320,128]{3,2,1,0:T(8,128)S(1)} copy-done((f32[2,2,320,128]{3,2,1,0:T(8,128)S(1)}, f32[2,2,320,128]{3,2,1,0:T(8,128)}, u32[]{:S(2)}) %copy-start) | copy-done | bytes 655384
  57.0 2.8 %shard_map.83 = bf16[576,128]{1,0:T(8,128)(2,1)} custom-call(bf16[4,576,128]{2,1,0:T(8,128)(2,1)S(1)} %bitcast.9, bf16[576,128]{1,0:T(8,128)(2,1)S(1)} %bitcast.10, bf16[1216,640]{1,0:T(8,128)(2,1)S(1)} %copy-done.1, bf16[128,512]{1,0:T(8,128)(2,1)S(1)} %copy-done.3, f32[2,2,320,128]{3,2,1,0:T(8,128)S(1)} %copy-done), custom_call_target="tpu_custom_call" | custom-call | tf_op jit(solution)/shard_map/pallas_call | solution.py:215
Async XLA Ops:
  0.0 20.9 %all-to-all-start = ((bf16[16,72,128]{2,1,0:T(8,128)(2,1)}), bf16[16,72,128]{2,1,0:T(8,128)(2,1)S(1)}, u32[]{:S(2)}, u32[]{:S(2)}) async-start(bf16[16,72,128]{2,1,0:T(8,128)(2,1)} %bitcast.11), calls=%async_computation | async-start | bytes 589824 | tf_op jit(solution)/shard_map/all_to_all | solution.py:250
  13.3 42.7 %copy-start.1 = (bf16[1216,640]{1,0:T(8,128)(2,1)S(1)}, bf16[1216,640]{1,0:T(8,128)(2,1)}, u32[]{:S(2)}) copy-start(bf16[1216,640]{1,0:T(8,128)(2,1)} %constant.43.clone.planes) | copy-start | bytes 4669444
  13.3 42.7 %copy-start.2 = (bf16[1,1,24,24,128]{4,3,2,1,0:T(8,128)(2,1)S(1)}, bf16[1,1,24,24,128]{4,3,2,1,0:T(8,128)(2,1)}, u32[]{:S(2)}) copy-start(bf16[1,1,24,24,128]{4,3,2,1,0:T(8,128)(2,1)} %param.8) | copy-start | bytes 442372
  13.3 42.7 %copy-start.3 = (bf16[128,512]{1,0:T(8,128)(2,1)S(1)}, bf16[128,512]{1,0:T(8,128)(2,1)}, u32[]{:S(2)}) copy-start(bf16[128,512]{1,0:T(8,128)(2,1)} %constant.44.clone.lines) | copy-start | bytes 393220
  13.3 12.6 %collective-permute-start = (s32[1,1]{1,0:T(1,128)}, s32[1,1]{1,0:T(1,128)}, u32[]{:S(2)}, u32[]{:S(2)}) collective-permute-start(s32[1,1]{1,0:T(1,128)} %bitcast.1), channel_id=1, source_target_pairs={{0,480},{1,449},{2,482},{3,451},{4,484},{5,453},{6,486},{7,455},{8... | collective-permute-start | bytes 20 | tf_op jit(solution)/shard_map/ppermute | solution.py:32
  26.6 9.0 %collective-permute-start.1 = (bf16[72,128]{1,0:T(8,128)(2,1)S(1)}, bf16[72,128]{1,0:T(8,128)(2,1)S(1)}, u32[]{:S(2)}, u32[]{:S(2)}) collective-permute-start(bf16[72,128]{1,0:T(8,128)(2,1)S(1)} %dynamic-slice_bitcast_fusion), channel_id=1, source_target_pairs={{0,32},{1,65},{2,34},{3,67},{4,36},{5,69},{6,38},{7,71},{8,40},{9,... | collective-permute-start | bytes 55304 | tf_op jit(solution)/shard_map/ppermute | solution.py:32
  36.3 14.0 %all-to-all-start.1 = ((bf16[16,72,128]{2,1,0:T(8,128)(2,1)}), bf16[16,72,128]{2,1,0:T(8,128)(2,1)S(1)}, u32[]{:S(2)}, u32[]{:S(2)}) async-start(bf16[16,72,128]{2,1,0:T(8,128)(2,1)} %broadcast_in_dim.2), calls=%async_computation.1 | async-start | bytes 589824 | tf_op jit(solution)/shard_map/all_to_all | solution.py:264
  56.0 1.1 %copy-start = (f32[2,2,320,128]{3,2,1,0:T(8,128)S(1)}, f32[2,2,320,128]{3,2,1,0:T(8,128)}, u32[]{:S(2)}) copy-start(f32[2,2,320,128]{3,2,1,0:T(8,128)} %shard_map.82.kern) | copy-start | bytes 1966084

commit v2 on v1

--- a/solution.py
+++ b/solution.py
@@ -71,17 +71,13 @@
 
 def plane_frequencies(grid_y, grid_z):
     chosen, opposite, differ = half_plane(grid_y, grid_z)
-    table = np.zeros((half_padded(grid_y, grid_z), 8), np.float32)
-    for column, (which, length) in enumerate(
-        [
-            (chosen // grid_z, grid_y),
-            (chosen % grid_z, grid_z),
-            (opposite // grid_z, grid_y),
-            (opposite % grid_z, grid_z),
-        ]
-    ):
-        table[: len(chosen), column] = np.where(which * 2 < length, which, which - length)
-    table[: len(chosen), 4] = differ
+    table = np.zeros((half_padded(grid_y, grid_z), LANES), np.float32)
+    for s in range(STEPS):
+        for sign, rows in enumerate((chosen, opposite)):
+            for axis, (which, length) in enumerate(((rows // grid_z, grid_y), (rows % grid_z, grid_z))):
+                signed = np.where(which * 2 < length, which, which - length)
+                table[: len(chosen), (axis * STEPS + s) * 2 + sign] = signed
+    table[: len(chosen), 4 * STEPS] = differ
     return table
 
 
@@ -94,53 +90,45 @@
     return np.concatenate([straight, turned], axis=1).astype(np.float32).astype(ml_dtypes.bfloat16)
 
 
-def coulomb_kernel(grid, wavevectors, umklapp, frequencies, out):
-    grid_x, grid_y, grid_z = grid
+def wave_square(signed, length, shift):
+    wavenumber = 2.0 * math.pi / (length * spacing) * (signed + shift)
+    return wavenumber * wavenumber
+
+
+def shifts_kernel(grid_x, wavevectors, umklapp, out):
     width = out.shape[-1]
-    cells = float(grid_x * grid_y * grid_z)
     k = lax.axis_index("ka")
     k_total = lax.axis_size("ka")
-
-    def square(signed, length, shift):
-        wavenumber = 2.0 * math.pi / (length * spacing) * (signed + shift)
-        return wavenumber * wavenumber
-
     lane = lax.broadcasted_iota(jnp.int32, (1, width), 1)
     index_x = jnp.where(lane < grid_x, lane, lane - grid_x)
     signed_x = jnp.where(index_x * 2 < grid_x, index_x, index_x - grid_x).astype(jnp.float32)
-    for s in range(out.shape[0]):
+    spread = jnp.zeros((1, width), jnp.float32)
+    out[...] = jnp.zeros_like(out)
+    for s in range(STEPS):
         visit = lax.rem(k + (k_total - s - 1), k_total)
         shift = [
             (wavevectors[a, k] - wavevectors[a, visit]).astype(jnp.float32) / KGRID
             + umklapp[0, s, a].astype(jnp.float32)
             for a in range(3)
         ]
-        line = square(signed_x, grid_x, shift[0])
-        kern = []
-        for column in (0, 2):
-            plane = square(frequencies[:, column : column + 1], grid_y, shift[1]) + square(
-                frequencies[:, column + 1 : column + 2], grid_z, shift[2]
-            )
-            kern.append((4.0 * math.pi / cells) / (plane + line + screening_sq))
-        opposite = kern[1] * frequencies[:, 4:5]
-        out[s, 0] = kern[0] + opposite
-        out[s, 1] = kern[0] - opposite
-
-
-def coulomb(wavevectors, umklapp, grid_x, grid_y, grid_z):
+        for axis in range(2):
+            spread = jnp.where(lane // 2 == axis * STEPS + s, shift[1 + axis], spread)
+        out[1 + s : 2 + s, :] = wave_square(signed_x, grid_x, shift[0]) + screening_sq
+    out[0:1, :] = spread
+
+
+def coulomb_shifts(wavevectors, umklapp, grid_x):
     smem = pl.BlockSpec(memory_space=pltpu.SMEM)
-    vmem = pl.BlockSpec(memory_space=pltpu.VMEM)
-    half = half_padded(grid_y, grid_z)
     return pl.pallas_call(
-        functools.partial(coulomb_kernel, (grid_x, grid_y, grid_z)),
-        out_shape=jax.ShapeDtypeStruct((STEPS, 2, half, 2 * grid_x), jnp.float32),
-        in_specs=[smem, smem, vmem],
-        out_specs=vmem,
-    )(wavevectors.T, umklapp, jnp.asarray(plane_frequencies(grid_y, grid_z)))
+        functools.partial(shifts_kernel, grid_x),
+        out_shape=jax.ShapeDtypeStruct((8, 2 * grid_x), jnp.float32),
+        in_specs=[smem, smem],
+        out_specs=pl.BlockSpec(memory_space=pltpu.VMEM),
+    )(wavevectors.T, umklapp)
 
 
 def exchange_kernel(
-    visitors, psi, planes, lines, kern, out, dense, given, even, odd, pair, stack, plane
+    grid, visitors, psi, planes, lines, frequencies, shifts, out, dense, given, even, odd, pair, stack, plane
 ):
     rows, turn = out.shape[0], LANES // 2
     width = planes.shape[1]
@@ -148,6 +136,21 @@
     terms = STEPS * OCC_DEV
     left = lax.broadcasted_iota(jnp.int32, (1, LANES), 1) < turn
     chunk = 96
+
+    grid_x, grid_y, grid_z = grid
+    cells = float(grid_x * grid_y * grid_z)
+    lane = lax.broadcasted_iota(jnp.int32, (1, LANES), 1)
+    length = jnp.where(lane < 2 * STEPS, float(grid_y), float(grid_z))
+
+    def coulomb(s):
+        squares = wave_square(frequencies[...], length, shifts[0:1, :])
+        squares = squares + pltpu.roll(squares, LANES - 2 * STEPS, 1)
+        kern = [
+            (4.0 * math.pi / cells) / (squares[:, at : at + 1] + shifts[1 + s : 2 + s, :])
+            for at in (2 * s, 2 * s + 1)
+        ]
+        opposite = kern[1] * frequencies[:, 4 * STEPS : 4 * STEPS + 1]
+        return kern[0] + opposite, kern[0] - opposite
 
     def lanes(term):
         return pl.ds(term * LANES, LANES)
@@ -176,7 +179,8 @@
     even[...] = jnp.dot(planes[:half], given[0], preferred_element_type=jnp.float32)
     odd[...] = jnp.dot(planes[half:width], given[1], preferred_element_type=jnp.float32)
     for term in range(terms):
-        total, differ = kern[term // OCC_DEV, 0], kern[term // OCC_DEV, 1]
+        if term % OCC_DEV == 0:
+            total, differ = coulomb(term // OCC_DEV)
         e, o = even[:, lanes(term)], odd[:, lanes(term)]
         pair[0, pl.ds(term * half, half), :] = (e * total + o * differ).astype(jnp.bfloat16)
         pair[1, pl.ds(term * half, half), :] = (e * differ + o * total).astype(jnp.bfloat16)
@@ -204,7 +208,7 @@
         out[pl.ds(first, chunk), :] = (prefactor * total).astype(out.dtype)
 
 
-def apply_exchange(visitors, psi, kern, grid_x, grid_y, grid_z):
+def apply_exchange(visitors, psi, shifts, grid_x, grid_y, grid_z):
     rows = grid_y * grid_z
     terms = STEPS * OCC_DEV
     planes = plane_tables(grid_y, grid_z)
@@ -213,9 +217,9 @@
     half = width // 2
     vmem = pl.BlockSpec(memory_space=pltpu.VMEM)
     return pl.pallas_call(
-        exchange_kernel,
+        functools.partial(exchange_kernel, (grid_x, grid_y, grid_z)),
         out_shape=jax.ShapeDtypeStruct((rows, LANES), jnp.bfloat16),
-        in_specs=[vmem] * 5,
+        in_specs=[vmem] * 6,
         out_specs=vmem,
         scratch_shapes=[
             pltpu.VMEM((terms * rows, LANES), jnp.bfloat16),
@@ -232,7 +236,8 @@
         psi,
         jnp.asarray(planes),
         jnp.asarray(lines),
-        kern,
+        jnp.asarray(plane_frequencies(grid_y, grid_z)),
+        shifts,
     )
 
 
@@ -248,18 +253,17 @@
 
     flat = occupied[0].reshape(n_yz, OCC_DEV * rows // n_yz, last_width)
     spread = lax.all_to_all(flat, "band", 0, 0, tiled=True, axis_index_groups=along_yz)
-    spread = lax.all_gather(spread, "band", axis_index_groups=cores)
-
-    places = jnp.bitwise_and(owners[0], 1) * n_yz + lax.shift_right_logical(owners[0], 1)
-    place = lax.dynamic_slice(places, (core, slot), (1, 1), allow_negative_indices=False)
-    wanted = shift_ka_by_core(place, -1)
+    spread = lax.all_gather(spread, "band", axis=1, axis_index_groups=cores)
+
+    owner = lax.dynamic_slice(owners[0], (core, slot), (1, 1), allow_negative_indices=False)
+    wanted = shift_ka_by_core(owner, -1)
     spread = spread.reshape((2 * n_yz,) + flat.shape[1:])
     chosen = lax.dynamic_slice(
         spread, (wanted[0, 0], 0, 0), (1,) + flat.shape[1:], allow_negative_indices=False
     )[0]
     mine = shift_ka_by_core(chosen, 1)
 
-    kern = coulomb(wavevectors, umklapp, grid_x, grid_y, grid_z)
+    shifts = coulomb_shifts(wavevectors, umklapp, grid_x)
     column = jnp.broadcast_to(mine[None], (n_yz,) + mine.shape)
     column = lax.all_to_all(column, "band", 0, 0, tiled=True, axis_index_groups=along_yz)
     visitors = lax.all_gather(column, "band", axis_index_groups=cores)
@@ -268,7 +272,7 @@
     result = apply_exchange(
         visitors,
         resident.reshape(rows, last_width),
-        kern,
+        shifts,
         grid_x,
         grid_y,
         grid_z,

time: 60.3 us -> 59.4 us (0.985)
  waiting for transfers between devices: 10.3 us -> 11.8 us
  Pallas kernels: 5.18 us -> 4.29 us
  starting transfers between devices: 30 us -> 29.2 us
  other arithmetic: 0.69 us -> 0 us
    all_to_all x1, waiting for transfers between devices: 5.89 us -> 6.88 us  [exchange(): lax.all_to_all(column, 'band', 0, 0, tiled=True, axis_index_groups=along_yz)]
    pallas_call x2, Pallas kernels: 5.18 us -> 4.29 us  [the longest x1 2.94 us: apply_exchange(): pl.pallas_call(functools.partial(exchange_kernel, (grid_x, grid_y, grid_z...]
    all_to_all x1, starting transfers between devices: 5.77 us -> 4.96 us  [exchange(): lax.all_to_all(column, 'band', 0, 0, tiled=True, axis_index_groups=along_yz)]
    add x1 -> x0, other arithmetic: 0.69 us -> none  [exchange(): jnp.bitwise_and(owners[0], 1) * n_yz + lax.shift_right_logical(owners[0], 1)]
  transfers between devices with their start and end apart: 4 -> 4, of which waited for: 2 -> 3; matrix products, arithmetic and copies ran while one was open for 2% -> 1% of each run, Pallas kernels for 4% -> 2%
where the time goes in v2:
time: 59.4 us; the launch traced here: 59 us
  starting transfers between devices  29.2 us (49%)
  waiting for transfers between devices  11.8 us (20%)
  blocking collectives  11 us (19%)
  Pallas kernels  4.29 us (7%)
  local copies, waits for them, and re-layouts  2.67 us (4%)
    all_to_all x1, starting transfers between devices, exchange(): lax.all_to_all(flat, 'band', 0, 0, tiled=True, axis_index_groups=along_yz)  12.1 us
    ppermute x2, starting transfers between devices, shift_ka_by_core(): return lax.ppermute(block, ('ka', 'band'), route)  12.1 us
    all_to_all x1, waiting for transfers between devices, exchange(): lax.all_to_all(column, 'band', 0, 0, tiled=True, axis_index_groups=along_yz)  6.88 us
    all_gather x1, blocking collectives, exchange(): visitors = lax.all_gather(column, 'band', axis_index_groups=cores)  5.61 us
    all_gather x1, blocking collectives, exchange(): spread = lax.all_gather(spread, 'band', axis=1, axis_index_groups=cores)  5.36 us
    all_to_all x1, starting transfers between devices, exchange(): lax.all_to_all(column, 'band', 0, 0, tiled=True, axis_index_groups=along_yz)  4.96 us
    ppermute x2, waiting for transfers between devices, shift_ka_by_core(): return lax.ppermute(block, ('ka', 'band'), route)  4.36 us
    pallas_call x1, Pallas kernels, apply_exchange(): pl.pallas_call(functools.partial(exchange_kernel, (grid_x, grid_y, grid_z...  2.94 us
  transfers between devices with their start and end apart: 4, of which 3 were waited for; matrix products, arithmetic and copies ran while one was open for 1% of the time, Pallas kernels for 2%

profile of v2, /device:TPU:1, one launch (start us, length us, event | category | flops | bytes accessed | tf_op | source)
XLA Modules:
  0.0 59.0 jit_solution(1379528472207418474)
XLA Ops:
  0.0 0.0 copy-start
  0.0 0.0 copy-start.1
  0.0 0.0 copy-start.2
  0.0 0.0 copy-start.3
  0.0 0.0 copy-start.4
  0.0 12.1 %all-to-all-start = ((bf16[16,72,128]{2,1,0:T(8,128)(2,1)}), bf16[16,72,128]{2,1,0:T(8,128)(2,1)S(1)}, u32[]{:S(2)}, u32[]{:S(2)}) async-start(bf16[16,72,128]{2,1,0:T(8,128)(2,1)} %bitcast.13), calls=%async_computation | async-start | bytes 589824 | tf_op jit(solution)/shard_map/all_to_all | solution.py:255
  12.2 0.0 copy-done
  12.2 0.6 constant_dynamic-slice_fusion
  12.8 7.4 %collective-permute-start = (s32[1,1]{1,0:T(1,128)}, s32[1,1]{1,0:T(1,128)}, u32[]{:S(2)}, u32[]{:S(2)}) collective-permute-start(s32[1,1]{1,0:T(1,128)} %bitcast.2), channel_id=1, source_target_pairs={{0,480},{1,449},{2,482},{3,451},{4,484},{5,453},{6,486},{7,455},{8... | collective-permute-start | bytes 20 | tf_op jit(solution)/shard_map/ppermute | solution.py:32
  20.2 0.5 all-to-all-done
  20.7 5.4 %all-gather = bf16[16,144,128]{2,1,0:T(8,128)(2,1)S(1)} all-gather(bf16[16,72,128]{2,1,0:T(8,128)(2,1)S(1)} %all-to-all-done), channel_id=2, replica_groups={{0,1},{2,3},{4,5},{6,7},{8,9},{10,11},{12,13},{14,15},{16,17},{18,19},{..., dimensions={1}, use_global_device_ids=true | all-gather | bytes 884736 | tf_op jit(solution)/shard_map/all_gather | solution.py:256
  26.1 0.0 collective-permute-done
  26.1 0.6 %dynamic-slice_bitcast_fusion = bf16[72,128]{1,0:T(8,128)(2,1)S(1)} fusion(bf16[32,72,128]{2,1,0:T(8,128)(2,1)S(1)} %bitcast.12, s32[]{:T(128)} %bitcast.3), kind=kLoop, calls=%fused_computation | loop fusion | bytes 36868 | tf_op jit(solution)/shard_map/squeeze | solution.py:261
  26.7 4.7 %collective-permute-start.1 = (bf16[72,128]{1,0:T(8,128)(2,1)S(1)}, bf16[72,128]{1,0:T(8,128)(2,1)S(1)}, u32[]{:S(2)}, u32[]{:S(2)}) collective-permute-start(bf16[72,128]{1,0:T(8,128)(2,1)S(1)} %dynamic-slice_bitcast_fusion), channel_id=1, source_target_pairs={{0,32},{1,65},{2,34},{3,67},{4,36},{5,69},{6,38},{7,71},{8,40},{9,... | collective-permute-start | bytes 55304 | tf_op jit(solution)/shard_map/ppermute | solution.py:32
  31.4 4.4 %collective-permute-done.1 = bf16[72,128]{1,0:T(8,128)(2,1)S(1)} collective-permute-done((bf16[72,128]{1,0:T(8,128)(2,1)S(1)}, bf16[72,128]{1,0:T(8,128)(2,1)S(1)}, u32[]{:S(2)}, u32[]{:S(2)}) %collective-permute-start.1) | collective-permute-done | bytes 18464 | tf_op jit(solution)/shard_map/ppermute | solution.py:32
  35.8 0.7 %broadcast_in_dim.2 = bf16[16,72,128]{2,1,0:T(8,128)(2,1)} broadcast(bf16[72,128]{1,0:T(8,128)(2,1)S(1)} %collective-permute-done.1), dimensions={1,2} | broadcast | bytes 313344 | tf_op jit(solution)/shard_map/broadcast_in_dim | solution.py:267
  36.5 5.0 %all-to-all-start.1 = ((bf16[16,72,128]{2,1,0:T(8,128)(2,1)}), bf16[16,72,128]{2,1,0:T(8,128)(2,1)S(1)}, u32[]{:S(2)}, u32[]{:S(2)}) async-start(bf16[16,72,128]{2,1,0:T(8,128)(2,1)} %broadcast_in_dim.2), calls=%async_computation.1 | async-start | bytes 589824 | tf_op jit(solution)/shard_map/all_to_all | solution.py:268
  41.5 1.3 %shard_map.82.shifts = f32[8,128]{1,0:T(8,128)} custom-call(s32[3,16]{1,0:T(4,128)} %bitcast.14, s32[1,2,3]{2,1,0:T(2,128)} %umklapp.1), custom_call_target="tpu_custom_call" | custom-call | tf_op jit(solution)/shard_map/pallas_call | solution.py:122
  42.8 6.9 %all-to-all-done.1 = bf16[16,72,128]{2,1,0:T(8,128)(2,1)S(1)} async-done(((bf16[16,72,128]{2,1,0:T(8,128)(2,1)}), bf16[16,72,128]{2,1,0:T(8,128)(2,1)S(1)}, u32[]{:S(2)}, u32[]{:S(2)}) %all-to-all-start.1) | async-done | bytes 294944 | tf_op jit(solution)/shard_map/all_to_all | solution.py:268
  49.7 5.6 %all-gather.1 = bf16[32,72,128]{2,1,0:T(8,128)(2,1)S(1)} all-gather(bf16[16,72,128]{2,1,0:T(8,128)(2,1)S(1)} %all-to-all-done.1), channel_id=3, replica_groups={{0,1},{2,3},{4,5},{6,7},{8,9},{10,11},{12,13},{14,15},{16,17},{18,19},{..., dimensions={0}, use_global_device_ids=true | all-gather | bytes 884736 | tf_op jit(solution)/shard_map/all_gather | solution.py:269
  55.3 0.0 copy-done.1
  55.3 0.0 copy-done.2
  55.3 0.0 copy-done.3
  55.3 0.0 copy-done.4
  55.3 0.0 copy-start.5
  55.3 0.7 %copy-done.5 = f32[8,128]{1,0:T(8,128)S(1)} copy-done((f32[8,128]{1,0:T(8,128)S(1)}, f32[8,128]{1,0:T(8,128)}, u32[]{:S(2)}) %copy-start.5) | copy-done | bytes 4120
  56.0 2.9 %shard_map.83 = bf16[576,128]{1,0:T(8,128)(2,1)} custom-call(bf16[4,576,128]{2,1,0:T(8,128)(2,1)S(1)} %bitcast.10, bf16[576,128]{1,0:T(8,128)(2,1)S(1)} %bitcast.11, bf16[1216,640]{1,0:T(8,128)(2,1)S(1)} %copy-done.1, bf16[128,512]{1,0:T(8,128)(2,1)S(1)} %copy-done.4, f32[320,128]{1,0:T(8,128)S(1)} %copy-done.2, f32[8,128]{1,0:T(8,128)S(1)} %copy-done.5), custom_call_target="tpu_custom_call" | custom-call | tf_op jit(solution)/shard_map/pallas_call | solution.py:219
Async XLA Ops:
  0.0 12.2 %copy-start = (s32[1,2,2]{2,1,0:T(2,128)S(1)}, s32[1,2,2]{2,1,0:T(2,128)}, u32[]{:S(2)}) copy-start(s32[1,2,2]{2,1,0:T(2,128)} %param.12) | copy-start | bytes 52
  0.0 55.3 %copy-start.1 = (bf16[1216,640]{1,0:T(8,128)(2,1)S(1)}, bf16[1216,640]{1,0:T(8,128)(2,1)}, u32[]{:S(2)}) copy-start(bf16[1216,640]{1,0:T(8,128)(2,1)} %constant.39.clone.planes) | copy-start | bytes 4669444
  0.0 55.3 %copy-start.2 = (f32[320,128]{1,0:T(8,128)S(1)}, f32[320,128]{1,0:T(8,128)}, u32[]{:S(2)}) copy-start(f32[320,128]{1,0:T(8,128)} %constant.41.clone.frequencies) | copy-start | bytes 491524
  0.0 55.3 %copy-start.3 = (bf16[1,1,24,24,128]{4,3,2,1,0:T(8,128)(2,1)S(1)}, bf16[1,1,24,24,128]{4,3,2,1,0:T(8,128)(2,1)}, u32[]{:S(2)}) copy-start(bf16[1,1,24,24,128]{4,3,2,1,0:T(8,128)(2,1)} %param.8) | copy-start | bytes 442372
  0.0 55.3 %copy-start.4 = (bf16[128,512]{1,0:T(8,128)(2,1)S(1)}, bf16[128,512]{1,0:T(8,128)(2,1)}, u32[]{:S(2)}) copy-start(bf16[128,512]{1,0:T(8,128)(2,1)} %constant.40.clone.lines) | copy-start | bytes 393220
  0.0 20.7 %all-to-all-start = ((bf16[16,72,128]{2,1,0:T(8,128)(2,1)}), bf16[16,72,128]{2,1,0:T(8,128)(2,1)S(1)}, u32[]{:S(2)}, u32[]{:S(2)}) async-start(bf16[16,72,128]{2,1,0:T(8,128)(2,1)} %bitcast.13), calls=%async_computation | async-start | bytes 589824 | tf_op jit(solution)/shard_map/all_to_all | solution.py:255
  12.8 13.3 %collective-permute-start = (s32[1,1]{1,0:T(1,128)}, s32[1,1]{1,0:T(1,128)}, u32[]{:S(2)}, u32[]{:S(2)}) collective-permute-start(s32[1,1]{1,0:T(1,128)} %bitcast.2), channel_id=1, source_target_pairs={{0,480},{1,449},{2,482},{3,451},{4,484},{5,453},{6,486},{7,455},{8... | collective-permute-start | bytes 20 | tf_op jit(solution)/shard_map/ppermute | solution.py:32
  26.7 9.0 %collective-permute-start.1 = (bf16[72,128]{1,0:T(8,128)(2,1)S(1)}, bf16[72,128]{1,0:T(8,128)(2,1)S(1)}, u32[]{:S(2)}, u32[]{:S(2)}) collective-permute-start(bf16[72,128]{1,0:T(8,128)(2,1)S(1)} %dynamic-slice_bitcast_fusion), channel_id=1, source_target_pairs={{0,32},{1,65},{2,34},{3,67},{4,36},{5,69},{6,38},{7,71},{8,40},{9,... | collective-permute-start | bytes 55304 | tf_op jit(solution)/shard_map/ppermute | solution.py:32
  36.5 13.2 %all-to-all-start.1 = ((bf16[16,72,128]{2,1,0:T(8,128)(2,1)}), bf16[16,72,128]{2,1,0:T(8,128)(2,1)S(1)}, u32[]{:S(2)}, u32[]{:S(2)}) async-start(bf16[16,72,128]{2,1,0:T(8,128)(2,1)} %broadcast_in_dim.2), calls=%async_computation.1 | async-start | bytes 589824 | tf_op jit(solution)/shard_map/all_to_all | solution.py:268
  55.3 0.7 %copy-start.5 = (f32[8,128]{1,0:T(8,128)S(1)}, f32[8,128]{1,0:T(8,128)}, u32[]{:S(2)}) copy-start(f32[8,128]{1,0:T(8,128)} %shard_map.82.shifts) | copy-start | bytes 12292

commit v3 on v2

--- a/solution.py
+++ b/solution.py
@@ -27,7 +27,7 @@
     route = []
     for k in range(n_ka):
         for b in range(n_band):
-            to = (k + sign * (1 + b % 2)) % n_ka
+            to = (k + sign * (STEPS - b % 2)) % n_ka
             route.append((k * n_band + b, to * n_band + b))
     return lax.ppermute(block, ("ka", "band"), route)
 
@@ -180,7 +180,7 @@
     odd[...] = jnp.dot(planes[half:width], given[1], preferred_element_type=jnp.float32)
     for term in range(terms):
         if term % OCC_DEV == 0:
-            total, differ = coulomb(term // OCC_DEV)
+            total, differ = coulomb(STEPS - 1 - term // OCC_DEV)
         e, o = even[:, lanes(term)], odd[:, lanes(term)]
         pair[0, pl.ds(term * half, half), :] = (e * total + o * differ).astype(jnp.bfloat16)
         pair[1, pl.ds(term * half, half), :] = (e * differ + o * total).astype(jnp.bfloat16)
@@ -255,7 +255,7 @@
     spread = lax.all_to_all(flat, "band", 0, 0, tiled=True, axis_index_groups=along_yz)
     spread = lax.all_gather(spread, "band", axis=1, axis_index_groups=cores)
 
-    owner = lax.dynamic_slice(owners[0], (core, slot), (1, 1), allow_negative_indices=False)
+    owner = lax.dynamic_slice(owners[0], (1 - core, slot), (1, 1), allow_negative_indices=False)
     wanted = shift_ka_by_core(owner, -1)
     spread = spread.reshape((2 * n_yz,) + flat.shape[1:])
     chosen = lax.dynamic_slice(

time: 59.4 us -> 59.4 us (level)
  starting transfers between devices: 29.2 us -> 27.6 us
  waiting for transfers between devices: 11.8 us -> 13 us
    ppermute x2, starting transfers between devices: 12.1 us -> 10.3 us  [shift_ka_by_core(): return lax.ppermute(block, ('ka', 'band'), route)]
    ppermute x2, waiting for transfers between devices: 4.36 us -> 5.6 us  [shift_ka_by_core(): return lax.ppermute(block, ('ka', 'band'), route)]
where the time goes in v3:
time: 59.4 us; the launch traced here: 59 us
  starting transfers between devices  27.6 us (46%)
  waiting for transfers between devices  13 us (22%)
  blocking collectives  11.3 us (19%)
  Pallas kernels  4.3 us (7%)
  local copies, waits for them, and re-layouts  2.67 us (4%)
    all_to_all x1, starting transfers between devices, exchange(): lax.all_to_all(flat, 'band', 0, 0, tiled=True, axis_index_groups=along_yz)  12.1 us
    ppermute x2, starting transfers between devices, shift_ka_by_core(): return lax.ppermute(block, ('ka', 'band'), route)  10.3 us
    all_to_all x1, waiting for transfers between devices, exchange(): lax.all_to_all(column, 'band', 0, 0, tiled=True, axis_index_groups=along_yz)  6.6 us
    all_gather x1, blocking collectives, exchange(): visitors = lax.all_gather(column, 'band', axis_index_groups=cores)  5.94 us
    ppermute x2, waiting for transfers between devices, shift_ka_by_core(): return lax.ppermute(block, ('ka', 'band'), route)  5.6 us
    all_gather x1, blocking collectives, exchange(): spread = lax.all_gather(spread, 'band', axis=1, axis_index_groups=cores)  5.36 us
    all_to_all x1, starting transfers between devices, exchange(): lax.all_to_all(column, 'band', 0, 0, tiled=True, axis_index_groups=along_yz)  5.22 us
    pallas_call x1, Pallas kernels, apply_exchange(): pl.pallas_call(functools.partial(exchange_kernel, (grid_x, grid_y, grid_z...  2.95 us
  transfers between devices with their start and end apart: 4, of which 3 were waited for; matrix products, arithmetic and copies ran while one was open for 1% of the time, Pallas kernels for 2%

profile of v3, /device:TPU:1, one launch (start us, length us, event | category | flops | bytes accessed | tf_op | source)
XLA Modules:
  0.0 59.0 jit_solution(4892729654100249371)
XLA Ops:
  0.0 0.0 copy-start
  0.0 0.0 copy-start.1
  0.0 0.0 copy-start.2
  0.0 0.0 copy-start.3
  0.0 0.0 copy-start.4
  0.0 12.1 %all-to-all-start = ((bf16[16,72,128]{2,1,0:T(8,128)(2,1)}), bf16[16,72,128]{2,1,0:T(8,128)(2,1)S(1)}, u32[]{:S(2)}, u32[]{:S(2)}) async-start(bf16[16,72,128]{2,1,0:T(8,128)(2,1)} %bitcast.13), calls=%async_computation | async-start | bytes 589824 | tf_op jit(solution)/shard_map/all_to_all | solution.py:255
  12.2 0.0 copy-done
  12.2 0.6 constant_dynamic-slice_fusion
  12.8 7.2 %collective-permute-start = (s32[1,1]{1,0:T(1,128)}, s32[1,1]{1,0:T(1,128)}, u32[]{:S(2)}, u32[]{:S(2)}) collective-permute-start(s32[1,1]{1,0:T(1,128)} %bitcast.2), channel_id=1, source_target_pairs={{0,448},{1,481},{2,450},{3,483},{4,452},{5,485},{6,454},{7,487},{8... | collective-permute-start | bytes 20 | tf_op jit(solution)/shard_map/ppermute | solution.py:32
  20.0 0.8 %all-to-all-done = bf16[16,72,128]{2,1,0:T(8,128)(2,1)S(1)} async-done(((bf16[16,72,128]{2,1,0:T(8,128)(2,1)}), bf16[16,72,128]{2,1,0:T(8,128)(2,1)S(1)}, u32[]{:S(2)}, u32[]{:S(2)}) %all-to-all-start) | async-done | bytes 294944 | tf_op jit(solution)/shard_map/all_to_all | solution.py:255
  20.7 5.4 %all-gather = bf16[16,144,128]{2,1,0:T(8,128)(2,1)S(1)} all-gather(bf16[16,72,128]{2,1,0:T(8,128)(2,1)S(1)} %all-to-all-done), channel_id=2, replica_groups={{0,1},{2,3},{4,5},{6,7},{8,9},{10,11},{12,13},{14,15},{16,17},{18,19},{..., dimensions={1}, use_global_device_ids=true | all-gather | bytes 884736 | tf_op jit(solution)/shard_map/all_gather | solution.py:256
  26.1 0.0 collective-permute-done
  26.1 0.6 %dynamic-slice_bitcast_fusion = bf16[72,128]{1,0:T(8,128)(2,1)S(1)} fusion(bf16[32,72,128]{2,1,0:T(8,128)(2,1)S(1)} %bitcast.12, s32[]{:T(128)} %bitcast.3), kind=kLoop, calls=%fused_computation | loop fusion | bytes 36868 | tf_op jit(solution)/shard_map/squeeze | solution.py:261
  26.7 3.1 %collective-permute-start.1 = (bf16[72,128]{1,0:T(8,128)(2,1)S(1)}, bf16[72,128]{1,0:T(8,128)(2,1)S(1)}, u32[]{:S(2)}, u32[]{:S(2)}) collective-permute-start(bf16[72,128]{1,0:T(8,128)(2,1)S(1)} %dynamic-slice_bitcast_fusion), channel_id=1, source_target_pairs={{0,64},{1,33},{2,66},{3,35},{4,68},{5,37},{6,70},{7,39},{8,72},{9,... | collective-permute-start | bytes 55304 | tf_op jit(solution)/shard_map/ppermute | solution.py:32
  29.9 5.6 %collective-permute-done.1 = bf16[72,128]{1,0:T(8,128)(2,1)S(1)} collective-permute-done((bf16[72,128]{1,0:T(8,128)(2,1)S(1)}, bf16[72,128]{1,0:T(8,128)(2,1)S(1)}, u32[]{:S(2)}, u32[]{:S(2)}) %collective-permute-start.1) | collective-permute-done | bytes 18464 | tf_op jit(solution)/shard_map/ppermute | solution.py:32
  35.5 0.7 %broadcast_in_dim.2 = bf16[16,72,128]{2,1,0:T(8,128)(2,1)} broadcast(bf16[72,128]{1,0:T(8,128)(2,1)S(1)} %collective-permute-done.1), dimensions={1,2} | broadcast | bytes 313344 | tf_op jit(solution)/shard_map/broadcast_in_dim | solution.py:267
  36.2 5.2 %all-to-all-start.1 = ((bf16[16,72,128]{2,1,0:T(8,128)(2,1)}), bf16[16,72,128]{2,1,0:T(8,128)(2,1)S(1)}, u32[]{:S(2)}, u32[]{:S(2)}) async-start(bf16[16,72,128]{2,1,0:T(8,128)(2,1)} %broadcast_in_dim.2), calls=%async_computation.1 | async-start | bytes 589824 | tf_op jit(solution)/shard_map/all_to_all | solution.py:268
  41.4 1.3 %shard_map.82.shifts = f32[8,128]{1,0:T(8,128)} custom-call(s32[3,16]{1,0:T(4,128)} %bitcast.14, s32[1,2,3]{2,1,0:T(2,128)} %umklapp.1), custom_call_target="tpu_custom_call" | custom-call | tf_op jit(solution)/shard_map/pallas_call | solution.py:122
  42.8 6.6 %all-to-all-done.1 = bf16[16,72,128]{2,1,0:T(8,128)(2,1)S(1)} async-done(((bf16[16,72,128]{2,1,0:T(8,128)(2,1)}), bf16[16,72,128]{2,1,0:T(8,128)(2,1)S(1)}, u32[]{:S(2)}, u32[]{:S(2)}) %all-to-all-start.1) | async-done | bytes 294944 | tf_op jit(solution)/shard_map/all_to_all | solution.py:268
  49.4 5.9 %all-gather.1 = bf16[32,72,128]{2,1,0:T(8,128)(2,1)S(1)} all-gather(bf16[16,72,128]{2,1,0:T(8,128)(2,1)S(1)} %all-to-all-done.1), channel_id=3, replica_groups={{0,1},{2,3},{4,5},{6,7},{8,9},{10,11},{12,13},{14,15},{16,17},{18,19},{..., dimensions={0}, use_global_device_ids=true | all-gather | bytes 884736 | tf_op jit(solution)/shard_map/all_gather | solution.py:269
  55.3 0.0 copy-done.1
  55.3 0.0 copy-done.2
  55.3 0.0 copy-done.3
  55.3 0.0 copy-done.4
  55.4 0.0 copy-start.5
  55.4 0.7 %copy-done.5 = f32[8,128]{1,0:T(8,128)S(1)} copy-done((f32[8,128]{1,0:T(8,128)S(1)}, f32[8,128]{1,0:T(8,128)}, u32[]{:S(2)}) %copy-start.5) | copy-done | bytes 4120
  56.0 3.0 %shard_map.83 = bf16[576,128]{1,0:T(8,128)(2,1)} custom-call(bf16[4,576,128]{2,1,0:T(8,128)(2,1)S(1)} %bitcast.10, bf16[576,128]{1,0:T(8,128)(2,1)S(1)} %bitcast.11, bf16[1216,640]{1,0:T(8,128)(2,1)S(1)} %copy-done.1, bf16[128,512]{1,0:T(8,128)(2,1)S(1)} %copy-done.4, f32[320,128]{1,0:T(8,128)S(1)} %copy-done.2, f32[8,128]{1,0:T(8,128)S(1)} %copy-done.5), custom_call_target="tpu_custom_call" | custom-call | tf_op jit(solution)/shard_map/pallas_call | solution.py:219
Async XLA Ops:
  0.0 12.2 %copy-start = (s32[1,2,2]{2,1,0:T(2,128)S(1)}, s32[1,2,2]{2,1,0:T(2,128)}, u32[]{:S(2)}) copy-start(s32[1,2,2]{2,1,0:T(2,128)} %param.12) | copy-start | bytes 52
  0.0 55.3 %copy-start.1 = (bf16[1216,640]{1,0:T(8,128)(2,1)S(1)}, bf16[1216,640]{1,0:T(8,128)(2,1)}, u32[]{:S(2)}) copy-start(bf16[1216,640]{1,0:T(8,128)(2,1)} %constant.40.clone.planes) | copy-start | bytes 4669444
  0.0 55.3 %copy-start.2 = (f32[320,128]{1,0:T(8,128)S(1)}, f32[320,128]{1,0:T(8,128)}, u32[]{:S(2)}) copy-start(f32[320,128]{1,0:T(8,128)} %constant.42.clone.frequencies) | copy-start | bytes 491524
  0.0 55.3 %copy-start.3 = (bf16[1,1,24,24,128]{4,3,2,1,0:T(8,128)(2,1)S(1)}, bf16[1,1,24,24,128]{4,3,2,1,0:T(8,128)(2,1)}, u32[]{:S(2)}) copy-start(bf16[1,1,24,24,128]{4,3,2,1,0:T(8,128)(2,1)} %param.8) | copy-start | bytes 442372
  0.0 55.3 %copy-start.4 = (bf16[128,512]{1,0:T(8,128)(2,1)S(1)}, bf16[128,512]{1,0:T(8,128)(2,1)}, u32[]{:S(2)}) copy-start(bf16[128,512]{1,0:T(8,128)(2,1)} %constant.41.clone.lines) | copy-start | bytes 393220
  0.0 20.7 %all-to-all-start = ((bf16[16,72,128]{2,1,0:T(8,128)(2,1)}), bf16[16,72,128]{2,1,0:T(8,128)(2,1)S(1)}, u32[]{:S(2)}, u32[]{:S(2)}) async-start(bf16[16,72,128]{2,1,0:T(8,128)(2,1)} %bitcast.13), calls=%async_computation | async-start | bytes 589824 | tf_op jit(solution)/shard_map/all_to_all | solution.py:255
  12.8 13.3 %collective-permute-start = (s32[1,1]{1,0:T(1,128)}, s32[1,1]{1,0:T(1,128)}, u32[]{:S(2)}, u32[]{:S(2)}) collective-permute-start(s32[1,1]{1,0:T(1,128)} %bitcast.2), channel_id=1, source_target_pairs={{0,448},{1,481},{2,450},{3,483},{4,452},{5,485},{6,454},{7,487},{8... | collective-permute-start | bytes 20 | tf_op jit(solution)/shard_map/ppermute | solution.py:32
  26.7 8.7 %collective-permute-start.1 = (bf16[72,128]{1,0:T(8,128)(2,1)S(1)}, bf16[72,128]{1,0:T(8,128)(2,1)S(1)}, u32[]{:S(2)}, u32[]{:S(2)}) collective-permute-start(bf16[72,128]{1,0:T(8,128)(2,1)S(1)} %dynamic-slice_bitcast_fusion), channel_id=1, source_target_pairs={{0,64},{1,33},{2,66},{3,35},{4,68},{5,37},{6,70},{7,39},{8,72},{9,... | collective-permute-start | bytes 55304 | tf_op jit(solution)/shard_map/ppermute | solution.py:32
  36.2 13.2 %all-to-all-start.1 = ((bf16[16,72,128]{2,1,0:T(8,128)(2,1)}), bf16[16,72,128]{2,1,0:T(8,128)(2,1)S(1)}, u32[]{:S(2)}, u32[]{:S(2)}) async-start(bf16[16,72,128]{2,1,0:T(8,128)(2,1)} %broadcast_in_dim.2), calls=%async_computation.1 | async-start | bytes 589824 | tf_op jit(solution)/shard_map/all_to_all | solution.py:268
  55.4 0.7 %copy-start.5 = (f32[8,128]{1,0:T(8,128)S(1)}, f32[8,128]{1,0:T(8,128)}, u32[]{:S(2)}) copy-start(f32[8,128]{1,0:T(8,128)} %shard_map.82.shifts) | copy-start | bytes 12292

commit v4 on v3

--- a/solution.py
+++ b/solution.py
@@ -164,8 +164,9 @@
         with_phi = jnp.where(left, own, -turned)
         with_turned = jnp.where(left, turned, own)
         for term in range(terms):
-            phi = visitors[term, pl.ds(first, chunk), :].astype(jnp.float32)
-            density = phi * with_phi + pltpu.roll(phi, turn, 1) * with_turned
+            phi = visitors[term, pl.ds(first, chunk), :]
+            other = pltpu.roll(phi, turn, 1).astype(jnp.float32)
+            density = phi.astype(jnp.float32) * with_phi + other * with_turned
             dense[pl.ds(term * rows + first, chunk), :] = density.astype(jnp.bfloat16)
     for term in range(terms):
         both = jnp.dot(
@@ -197,9 +198,10 @@
     for first in range(0, rows, chunk):
         straight = crossed = None
         for term in range(terms):
-            phi = visitors[term, pl.ds(first, chunk), :].astype(jnp.float32)
+            phi = visitors[term, pl.ds(first, chunk), :]
+            other = pltpu.roll(phi, turn, 1).astype(jnp.float32)
             potential = plane[pl.ds(first, chunk), lanes(term)]
-            one, two = phi * potential, pltpu.roll(phi, turn, 1) * potential
+            one, two = phi.astype(jnp.float32) * potential, other * potential
             straight = one if term == 0 else straight + one
             crossed = two if term == 0 else crossed + two
         total = jnp.where(

time: 59.4 us -> 59.4 us (level)
  no operation moved by 1% of the time
where the time goes in v4:
time: 59.4 us; the launch traced here: 59 us
  starting transfers between devices  27.6 us (46%)
  waiting for transfers between devices  13 us (22%)
  blocking collectives  11.3 us (19%)
  Pallas kernels  4.29 us (7%)
  local copies, waits for them, and re-layouts  2.67 us (4%)
    all_to_all x1, starting transfers between devices, exchange(): lax.all_to_all(flat, 'band', 0, 0, tiled=True, axis_index_groups=along_yz)  12.1 us
    ppermute x2, starting transfers between devices, shift_ka_by_core(): return lax.ppermute(block, ('ka', 'band'), route)  10.3 us
    all_to_all x1, waiting for transfers between devices, exchange(): lax.all_to_all(column, 'band', 0, 0, tiled=True, axis_index_groups=along_yz)  6.6 us
    all_gather x1, blocking collectives, exchange(): visitors = lax.all_gather(column, 'band', axis_index_groups=cores)  5.94 us
    ppermute x2, waiting for transfers between devices, shift_ka_by_core(): return lax.ppermute(block, ('ka', 'band'), route)  5.6 us
    all_gather x1, blocking collectives, exchange(): spread = lax.all_gather(spread, 'band', axis=1, axis_index_groups=cores)  5.36 us
    all_to_all x1, starting transfers between devices, exchange(): lax.all_to_all(column, 'band', 0, 0, tiled=True, axis_index_groups=along_yz)  5.22 us
    pallas_call x1, Pallas kernels, apply_exchange(): pl.pallas_call(functools.partial(exchange_kernel, (grid_x, grid_y, grid_z...  2.94 us
  transfers between devices with their start and end apart: 4, of which 3 were waited for; matrix products, arithmetic and copies ran while one was open for 1% of the time, Pallas kernels for 2%

profile of v4, /device:TPU:1, one launch (start us, length us, event | category | flops | bytes accessed | tf_op | source)
XLA Modules:
  0.0 59.0 jit_solution(4430339645211619990)
XLA Ops:
  0.0 0.0 copy-start
  0.0 0.0 copy-start.1
  0.0 0.0 copy-start.2
  0.0 0.0 copy-start.3
  0.0 0.0 copy-start.4
  0.0 12.1 %all-to-all-start = ((bf16[16,72,128]{2,1,0:T(8,128)(2,1)}), bf16[16,72,128]{2,1,0:T(8,128)(2,1)S(1)}, u32[]{:S(2)}, u32[]{:S(2)}) async-start(bf16[16,72,128]{2,1,0:T(8,128)(2,1)} %bitcast.13), calls=%async_computation | async-start | bytes 589824 | tf_op jit(solution)/shard_map/all_to_all | solution.py:257
  12.2 0.0 copy-done
  12.2 0.6 constant_dynamic-slice_fusion
  12.8 7.2 %collective-permute-start = (s32[1,1]{1,0:T(1,128)}, s32[1,1]{1,0:T(1,128)}, u32[]{:S(2)}, u32[]{:S(2)}) collective-permute-start(s32[1,1]{1,0:T(1,128)} %bitcast.2), channel_id=1, source_target_pairs={{0,448},{1,481},{2,450},{3,483},{4,452},{5,485},{6,454},{7,487},{8... | collective-permute-start | bytes 20 | tf_op jit(solution)/shard_map/ppermute | solution.py:32
  20.0 0.8 %all-to-all-done = bf16[16,72,128]{2,1,0:T(8,128)(2,1)S(1)} async-done(((bf16[16,72,128]{2,1,0:T(8,128)(2,1)}), bf16[16,72,128]{2,1,0:T(8,128)(2,1)S(1)}, u32[]{:S(2)}, u32[]{:S(2)}) %all-to-all-start) | async-done | bytes 294944 | tf_op jit(solution)/shard_map/all_to_all | solution.py:257
  20.7 5.4 %all-gather = bf16[16,144,128]{2,1,0:T(8,128)(2,1)S(1)} all-gather(bf16[16,72,128]{2,1,0:T(8,128)(2,1)S(1)} %all-to-all-done), channel_id=2, replica_groups={{0,1},{2,3},{4,5},{6,7},{8,9},{10,11},{12,13},{14,15},{16,17},{18,19},{..., dimensions={1}, use_global_device_ids=true | all-gather | bytes 884736 | tf_op jit(solution)/shard_map/all_gather | solution.py:258
  26.1 0.0 collective-permute-done
  26.1 0.6 %dynamic-slice_bitcast_fusion = bf16[72,128]{1,0:T(8,128)(2,1)S(1)} fusion(bf16[32,72,128]{2,1,0:T(8,128)(2,1)S(1)} %bitcast.12, s32[]{:T(128)} %bitcast.3), kind=kLoop, calls=%fused_computation | loop fusion | bytes 36868 | tf_op jit(solution)/shard_map/squeeze | solution.py:263
  26.7 3.1 %collective-permute-start.1 = (bf16[72,128]{1,0:T(8,128)(2,1)S(1)}, bf16[72,128]{1,0:T(8,128)(2,1)S(1)}, u32[]{:S(2)}, u32[]{:S(2)}) collective-permute-start(bf16[72,128]{1,0:T(8,128)(2,1)S(1)} %dynamic-slice_bitcast_fusion), channel_id=1, source_target_pairs={{0,64},{1,33},{2,66},{3,35},{4,68},{5,37},{6,70},{7,39},{8,72},{9,... | collective-permute-start | bytes 55304 | tf_op jit(solution)/shard_map/ppermute | solution.py:32
  29.9 5.6 %collective-permute-done.1 = bf16[72,128]{1,0:T(8,128)(2,1)S(1)} collective-permute-done((bf16[72,128]{1,0:T(8,128)(2,1)S(1)}, bf16[72,128]{1,0:T(8,128)(2,1)S(1)}, u32[]{:S(2)}, u32[]{:S(2)}) %collective-permute-start.1) | collective-permute-done | bytes 18464 | tf_op jit(solution)/shard_map/ppermute | solution.py:32
  35.5 0.7 %broadcast_in_dim.2 = bf16[16,72,128]{2,1,0:T(8,128)(2,1)} broadcast(bf16[72,128]{1,0:T(8,128)(2,1)S(1)} %collective-permute-done.1), dimensions={1,2} | broadcast | bytes 313344 | tf_op jit(solution)/shard_map/broadcast_in_dim | solution.py:269
  36.2 5.2 %all-to-all-start.1 = ((bf16[16,72,128]{2,1,0:T(8,128)(2,1)}), bf16[16,72,128]{2,1,0:T(8,128)(2,1)S(1)}, u32[]{:S(2)}, u32[]{:S(2)}) async-start(bf16[16,72,128]{2,1,0:T(8,128)(2,1)} %broadcast_in_dim.2), calls=%async_computation.1 | async-start | bytes 589824 | tf_op jit(solution)/shard_map/all_to_all | solution.py:270
  41.4 1.3 %shard_map.82.shifts = f32[8,128]{1,0:T(8,128)} custom-call(s32[3,16]{1,0:T(4,128)} %bitcast.14, s32[1,2,3]{2,1,0:T(2,128)} %umklapp.1), custom_call_target="tpu_custom_call" | custom-call | tf_op jit(solution)/shard_map/pallas_call | solution.py:122
  42.8 6.6 %all-to-all-done.1 = bf16[16,72,128]{2,1,0:T(8,128)(2,1)S(1)} async-done(((bf16[16,72,128]{2,1,0:T(8,128)(2,1)}), bf16[16,72,128]{2,1,0:T(8,128)(2,1)S(1)}, u32[]{:S(2)}, u32[]{:S(2)}) %all-to-all-start.1) | async-done | bytes 294944 | tf_op jit(solution)/shard_map/all_to_all | solution.py:270
  49.4 5.9 %all-gather.1 = bf16[32,72,128]{2,1,0:T(8,128)(2,1)S(1)} all-gather(bf16[16,72,128]{2,1,0:T(8,128)(2,1)S(1)} %all-to-all-done.1), channel_id=3, replica_groups={{0,1},{2,3},{4,5},{6,7},{8,9},{10,11},{12,13},{14,15},{16,17},{18,19},{..., dimensions={0}, use_global_device_ids=true | all-gather | bytes 884736 | tf_op jit(solution)/shard_map/all_gather | solution.py:271
  55.3 0.0 copy-done.1
  55.3 0.0 copy-done.2
  55.3 0.0 copy-done.3
  55.3 0.0 copy-done.4
  55.4 0.0 copy-start.5
  55.4 0.7 %copy-done.5 = f32[8,128]{1,0:T(8,128)S(1)} copy-done((f32[8,128]{1,0:T(8,128)S(1)}, f32[8,128]{1,0:T(8,128)}, u32[]{:S(2)}) %copy-start.5) | copy-done | bytes 4120
  56.0 2.9 %shard_map.83 = bf16[576,128]{1,0:T(8,128)(2,1)} custom-call(bf16[4,576,128]{2,1,0:T(8,128)(2,1)S(1)} %bitcast.10, bf16[576,128]{1,0:T(8,128)(2,1)S(1)} %bitcast.11, bf16[1216,640]{1,0:T(8,128)(2,1)S(1)} %copy-done.1, bf16[128,512]{1,0:T(8,128)(2,1)S(1)} %copy-done.4, f32[320,128]{1,0:T(8,128)S(1)} %copy-done.2, f32[8,128]{1,0:T(8,128)S(1)} %copy-done.5), custom_call_target="tpu_custom_call" | custom-call | tf_op jit(solution)/shard_map/pallas_call | solution.py:221
Async XLA Ops:
  0.0 12.2 %copy-start = (s32[1,2,2]{2,1,0:T(2,128)S(1)}, s32[1,2,2]{2,1,0:T(2,128)}, u32[]{:S(2)}) copy-start(s32[1,2,2]{2,1,0:T(2,128)} %param.12) | copy-start | bytes 52
  0.0 55.3 %copy-start.1 = (bf16[1216,640]{1,0:T(8,128)(2,1)S(1)}, bf16[1216,640]{1,0:T(8,128)(2,1)}, u32[]{:S(2)}) copy-start(bf16[1216,640]{1,0:T(8,128)(2,1)} %constant.40.clone.planes) | copy-start | bytes 4669444
  0.0 55.3 %copy-start.2 = (f32[320,128]{1,0:T(8,128)S(1)}, f32[320,128]{1,0:T(8,128)}, u32[]{:S(2)}) copy-start(f32[320,128]{1,0:T(8,128)} %constant.42.clone.frequencies) | copy-start | bytes 491524
  0.0 55.3 %copy-start.3 = (bf16[1,1,24,24,128]{4,3,2,1,0:T(8,128)(2,1)S(1)}, bf16[1,1,24,24,128]{4,3,2,1,0:T(8,128)(2,1)}, u32[]{:S(2)}) copy-start(bf16[1,1,24,24,128]{4,3,2,1,0:T(8,128)(2,1)} %param.8) | copy-start | bytes 442372
  0.0 55.3 %copy-start.4 = (bf16[128,512]{1,0:T(8,128)(2,1)S(1)}, bf16[128,512]{1,0:T(8,128)(2,1)}, u32[]{:S(2)}) copy-start(bf16[128,512]{1,0:T(8,128)(2,1)} %constant.41.clone.lines) | copy-start | bytes 393220
  0.0 20.7 %all-to-all-start = ((bf16[16,72,128]{2,1,0:T(8,128)(2,1)}), bf16[16,72,128]{2,1,0:T(8,128)(2,1)S(1)}, u32[]{:S(2)}, u32[]{:S(2)}) async-start(bf16[16,72,128]{2,1,0:T(8,128)(2,1)} %bitcast.13), calls=%async_computation | async-start | bytes 589824 | tf_op jit(solution)/shard_map/all_to_all | solution.py:257
  12.8 13.3 %collective-permute-start = (s32[1,1]{1,0:T(1,128)}, s32[1,1]{1,0:T(1,128)}, u32[]{:S(2)}, u32[]{:S(2)}) collective-permute-start(s32[1,1]{1,0:T(1,128)} %bitcast.2), channel_id=1, source_target_pairs={{0,448},{1,481},{2,450},{3,483},{4,452},{5,485},{6,454},{7,487},{8... | collective-permute-start | bytes 20 | tf_op jit(solution)/shard_map/ppermute | solution.py:32
  26.7 8.7 %collective-permute-start.1 = (bf16[72,128]{1,0:T(8,128)(2,1)S(1)}, bf16[72,128]{1,0:T(8,128)(2,1)S(1)}, u32[]{:S(2)}, u32[]{:S(2)}) collective-permute-start(bf16[72,128]{1,0:T(8,128)(2,1)S(1)} %dynamic-slice_bitcast_fusion), channel_id=1, source_target_pairs={{0,64},{1,33},{2,66},{3,35},{4,68},{5,37},{6,70},{7,39},{8,72},{9,... | collective-permute-start | bytes 55304 | tf_op jit(solution)/shard_map/ppermute | solution.py:32
  36.2 13.2 %all-to-all-start.1 = ((bf16[16,72,128]{2,1,0:T(8,128)(2,1)}), bf16[16,72,128]{2,1,0:T(8,128)(2,1)S(1)}, u32[]{:S(2)}, u32[]{:S(2)}) async-start(bf16[16,72,128]{2,1,0:T(8,128)(2,1)} %broadcast_in_dim.2), calls=%async_computation.1 | async-start | bytes 589824 | tf_op jit(solution)/shard_map/all_to_all | solution.py:270
  55.4 0.7 %copy-start.5 = (f32[8,128]{1,0:T(8,128)S(1)}, f32[8,128]{1,0:T(8,128)}, u32[]{:S(2)}) copy-start(f32[8,128]{1,0:T(8,128)} %shard_map.82.shifts) | copy-start | bytes 12292
